TPU v7x, 32 devices: a whole 2x2x4 slice. The times are simulated.
32 devices in a mesh: rep: 1, fsdp: 32 (over z, y, x, core).
Axes of the slice: x: 2, y: 2, z: 4, core: 2. Of those that a mesh axis runs over, the one named last changes fastest.
Arguments:
- accumulated: bfloat16 [1, 2048, 14336], P('rep', 'fsdp'), may hold values from -6 to 6
- q_start: bfloat16 [32, 14336], P(None, 'fsdp'), may hold values from -6 to 6
Outputs:
- residual_buffer: bfloat16 [1, 2048, 14336], P('rep', 'fsdp')
- basis_f32: float32 [2048, 32], P('fsdp')
- q_factor: float32 [32, 14336], P(None, 'fsdp')
All inputs are finite; a program needn't handle non-finite values.
Results may differ from a plain program's by a relative error of at most 0.0039.
Values may be sent and summed in bfloat16 or wider, within the bound.
No kernel may reach another device: no remote copies, remote signals or barrier semaphores. Data moves between devices by JAX's collectives and lax.ppermute only.
A program may use at most 64 MiB of HBM per device.

v0:
```python
import jax
import jax.numpy as jnp
from jax import lax
from jax.sharding import PartitionSpec as P

ITERS = 2


def orthonormal(p_sum):
    partial_gram = jnp.dot(p_sum.T, p_sum, precision=lax.Precision.HIGHEST)
    gram_matrix = lax.psum(partial_gram, "fsdp")
    factor = jnp.linalg.cholesky(gram_matrix)
    return lax.linalg.triangular_solve(factor, p_sum, left_side=False, lower=True, transpose_a=True)


def on_device(accumulated, q_start):
    own_rows = accumulated[0]
    replicas = lax.axis_size("rep")
    shard_cols = q_start.shape[1]
    owner_offset = lax.axis_index("fsdp") * shard_cols
    right_factor = q_start
    for iteration in range(ITERS):
        if iteration == 0:
            term = lax.dot_general(
                own_rows,
                lax.all_gather(q_start, "fsdp", axis=1, tiled=True),
                (((1,), (1,)), ((), ())),
                preferred_element_type=jnp.float32,
            )
            p_local = term
        else:
            p_local = lax.dot_general(
                own_rows, right_factor, (((1,), (1,)), ((), ())), preferred_element_type=jnp.float32
            )
        p_sum = lax.psum(p_local, "rep")
        basis_f32 = orthonormal(p_sum)
        basis_bf16 = basis_f32.astype(jnp.bfloat16)
        q_term = lax.dot_general(
            basis_bf16, own_rows, (((0,), (0,)), ((), ())), preferred_element_type=jnp.float32
        )
        q_whole = lax.psum(q_term, ("rep", "fsdp")) / replicas
        q_owned = lax.dynamic_slice_in_dim(q_whole, owner_offset, shard_cols, 1)
        right_factor = q_whole.astype(jnp.bfloat16)
    approx = lax.dot_general(
        basis_bf16, right_factor, (((1,), (0,)), ((), ())), preferred_element_type=jnp.float32
    )
    residual_buffer = (own_rows.astype(jnp.float32) - approx).astype(jnp.bfloat16)[None]
    return (residual_buffer, basis_f32, q_owned)


def solution(mesh):
    in_specs = (P("rep", "fsdp", None), P(None, "fsdp"))
    out_specs = (P("rep", "fsdp", None), P("fsdp", None), P(None, "fsdp"))
    return jax.shard_map(
        on_device, mesh=mesh, in_specs=in_specs, out_specs=out_specs, check_vma=False
    )
```

profile of v0, /device:TPU:0, one launch (start us, length us, event | category | flops | bytes accessed | tf_op | source)
XLA Modules:
  0.0 356.6 jit_solution(10952083144412553600)
XLA Ops:
  7.2 46.5 %all-gather = bf16[32,448,32]{1,2,0:T(8,128)(2,1)S(1)} all-gather(bf16[1,448,32]{1,2,0:T(8,128)(2,1)} %bitcast.52), channel_id=1, replica_groups=mesh['rep'=1,'fsdp'=32] {'fsdp'}, dimensions={0}, use_global_device_ids=true | all-gather | bytes 946176 | tf_op jit(solution)/shard_map/all_gather | solution.py:26
  53.7 0.6 copy.14
  54.2 2.1 reshape.20
  56.4 1.8 fusion.8
  58.3 36.9 %psum.26 = f32[32,32]{0,1:T(8,128)S(1)} all-reduce(f32[32,32]{0,1:T(8,128)S(1)} %fusion.24), channel_id=1, replica_groups=mesh['rep'=1,'fsdp'=32] {'fsdp'}, use_global_device_ids=true, to_apply=%region_0.0 | all-reduce | flops 1024 | bytes 8192 | tf_op jit(solution)/shard_map/psum | solution.py:11
  95.3 2.9 cholesky.44
  98.3 0.6 compare_reduce_fusion.1
  98.9 0.7 fusion.13
  99.6 2.4 custom-call.6
  102.0 0.2 fusion.10
  102.3 1.6 fusion.6
  103.9 59.3 %all-reduce.4 = bf16[32,14336]{1,0:T(8,128)(2,1)S(1)} all-reduce(f32[32,14336]{1,0:T(8,128)} %fusion.6), channel_id=1, replica_groups=mesh['rep'=1,'fsdp'=32] {'rep','fsdp'}, use_global_device_ids=true, to_apply=%region_3.6 | all-reduce | flops 458752 | bytes 2752512 | tf_op jit(solution)/shard_map/psum | solution.py:41
  163.2 0.6 fusion.4
  163.8 0.2 fusion.25
  164.0 37.5 %psum.36 = f32[32,32]{0,1:T(8,128)S(1)} all-reduce(f32[32,32]{0,1:T(8,128)S(1)} %fusion.25), channel_id=1, replica_groups=mesh['rep'=1,'fsdp'=32] {'fsdp'}, use_global_device_ids=true, to_apply=%region_4.7 | all-reduce | flops 1024 | bytes 8192 | tf_op jit(solution)/shard_map/psum | solution.py:11
  201.5 2.9 cholesky.55
  204.5 0.6 compare_reduce_fusion
  205.1 0.7 fusion.14
  205.8 2.4 custom-call.7
  208.2 0.2 convolution_bitcast_fusion
  208.5 1.6 fusion.2
  210.1 134.6 %all-reduce.3.cloned.1.call-done = f32[32,14336]{1,0:T(8,128)} async-done(((f32[32,14336]{1,0:T(8,128)}), f32[32,14336]{1,0:T(8,128)}) %all-reduce.3.cloned.1.call-update) | async-done | bytes 1835024 | tf_op jit(solution)/shard_map/psum | solution.py:41
  344.7 3.4 fusion.1
  348.1 1.6 constant_dynamic-slice_fusion
  (13 shorter events, 0.4 us)
Async XLA Ops:
  7.2 337.6 %all-reduce.3.cloned.1.call-start = ((), (), s32[]{:S(2)}) async-start(), calls=%async_computation | async-start | bytes 3670016 | tf_op jit(solution)/shard_map/psum | solution.py:41
  53.7 2.7 copy-start
  208.5 136.3 %copy-start.1 = (f32[64,32]{0,1:T(8,128)}, f32[64,32]{0,1:T(8,128)S(1)}, u32[]{:S(2)}) copy-start(f32[64,32]{0,1:T(8,128)S(1)} %convolution_bitcast_fusion) | copy-start | bytes 24580
Sparse Core Ops, SparseCore 0:
  210.2 134.4 all-reduce.2
where the time goes:
time: 357 us
  blocking collectives  180 us (50%)
  waiting for transfers between devices  135 us (38%)
  between operations  14.1 us (4%)
  other arithmetic  13.4 us (4%)
  matrix products  9.79 us (3%)
  local copies, waits for them, and re-layouts  4.44 us (1%)
    psum x1, waiting for transfers between devices, on_device(): q_whole = lax.psum(q_term, ('rep', 'fsdp')) / replicas  135 us
    psum x2, blocking collectives, orthonormal(): gram_matrix = lax.psum(partial_gram, 'fsdp')  74.4 us
    psum x1, blocking collectives, on_device(): q_whole = lax.psum(q_term, ('rep', 'fsdp')) / replicas  59.3 us
    all_gather x1, blocking collectives, on_device(): lax.all_gather(q_start, 'fsdp', axis=1, tiled=True)  46.5 us
    another operation x6, other arithmetic, orthonormal(): factor = jnp.linalg.cholesky(gram_matrix)  7.19 us
  transfers between devices with their start and end apart: 1, of which 1 were waited for; matrix products, arithmetic and copies ran while one was open for 0% of the time, Pallas kernels for 0%

commit v1 on v0

--- a/solution.py
+++ b/solution.py
@@ -1,9 +1,19 @@
+import functools
 import jax
 import jax.numpy as jnp
 from jax import lax
 from jax.sharding import PartitionSpec as P
+from jax.lax import all_gather
 
 ITERS = 2
+
+
+def try_all_tiles(inputs, mesh_ax):
+    y_new = jnp.sum(all_gather(inputs, mesh_ax), 0)
+    return y_new
+
+
+try_all_the_axis_part = functools.partial(try_all_tiles, mesh_ax=("rep", "fsdp"))
 
 
 def orthonormal(p_sum):
@@ -38,7 +48,7 @@
         q_term = lax.dot_general(
             basis_bf16, own_rows, (((0,), (0,)), ((), ())), preferred_element_type=jnp.float32
         )
-        q_whole = lax.psum(q_term, ("rep", "fsdp")) / replicas
+        q_whole = try_all_the_axis_part(q_term) / replicas
         q_owned = lax.dynamic_slice_in_dim(q_whole, owner_offset, shard_cols, 1)
         right_factor = q_whole.astype(jnp.bfloat16)
     approx = lax.dot_general(

time: 357 us -> 834 us (2.34)
  waiting for transfers between devices: 135 us -> 632 us
  blocking collectives: 180 us -> 122 us
  other arithmetic: 13.4 us -> 51.5 us
    all_gather x0 -> x2, waiting for transfers between devices: none -> 632 us  [try_all_tiles(): y_new = jnp.sum(all_gather(inputs, mesh_ax), 0)]
    psum x1 -> x0, waiting for transfers between devices: 135 us -> none  [on_device(): q_whole = lax.psum(q_term, ('rep', 'fsdp')) / replicas]
    psum x1 -> x0, blocking collectives: 59.3 us -> none  [on_device(): q_whole = lax.psum(q_term, ('rep', 'fsdp')) / replicas]
    reduce_sum x0 -> x2, other arithmetic: none -> 38.1 us  [try_all_tiles(): y_new = jnp.sum(all_gather(inputs, mesh_ax), 0)]
  transfers between devices with their start and end apart: 1 -> 2, of which waited for: 1 -> 2; matrix products, arithmetic and copies ran while one was open for 0% -> 0% of each run, Pallas kernels for 0% -> 0%
where the time goes in v1:
time: 834 us; the launch traced here: 833 us
  waiting for transfers between devices  632 us (76%)
  blocking collectives  122 us (15%)
  other arithmetic  51.5 us (6%)
  between operations  14.1 us (2%)
  matrix products  9.79 us (1%)
    all_gather x2, waiting for transfers between devices, try_all_tiles(): y_new = jnp.sum(all_gather(inputs, mesh_ax), 0)  632 us
    psum x2, blocking collectives, orthonormal(): gram_matrix = lax.psum(partial_gram, 'fsdp')  75.4 us
    all_gather x1, blocking collectives, on_device(): lax.all_gather(q_start, 'fsdp', axis=1, tiled=True)  46.5 us
    reduce_sum x2, other arithmetic, try_all_tiles(): y_new = jnp.sum(all_gather(inputs, mesh_ax), 0)  38.1 us
  transfers between devices with their start and end apart: 2, of which 2 were waited for; matrix products, arithmetic and copies ran while one was open for 0% of the time, Pallas kernels for 0%

profile of v1, /device:TPU:0, one launch (start us, length us, event | category | flops | bytes accessed | tf_op | source)
XLA Modules:
  0.0 833.4 jit_solution(1532268846572069883)
XLA Ops:
  7.2 46.5 %all-gather.2 = bf16[32,448,32]{1,2,0:T(8,128)(2,1)S(1)} all-gather(bf16[1,448,32]{1,2,0:T(8,128)(2,1)} %bitcast.56), channel_id=1, replica_groups=mesh['rep'=1,'fsdp'=32] {'fsdp'}, dimensions={0}, use_global_device_ids=true | all-gather | bytes 946176 | tf_op jit(solution)/shard_map/all_gather | solution.py:36
  53.7 0.6 copy.14
  54.2 2.1 reshape.22
  56.4 1.8 fusion.8
  58.3 36.9 %psum.14 = f32[32,32]{0,1:T(8,128)S(1)} all-reduce(f32[32,32]{0,1:T(8,128)S(1)} %fusion.24), channel_id=1, replica_groups=mesh['rep'=1,'fsdp'=32] {'fsdp'}, use_global_device_ids=true, to_apply=%region_0.0 | all-reduce | flops 1024 | bytes 8192 | tf_op jit(solution)/shard_map/psum | solution.py:21
  95.3 2.9 cholesky.44
  98.3 0.6 compare_reduce_fusion.1
  98.9 0.7 fusion.13
  99.6 2.4 custom-call.6
  102.0 0.2 fusion.10
  102.2 1.6 fusion.6
  103.9 315.6 %all-gather.6.cloned.1.call-done = f32[1024,14336]{1,0:T(8,128)} async-done(((f32[32,14336]{1,0:T(8,128)}), f32[1024,14336]{1,0:T(8,128)}) %all-gather.6.cloned.1.call-update) | async-done | bytes 58720272 | tf_op jit(solution)/shard_map/all_gather | solution.py:12
  419.6 18.5 %reduce_sum.18 = bf16[32,14336]{1,0:T(8,128)(2,1)S(1)} reduce(f32[32,32,14336]{2,1,0:T(8,128)} %bitcast.55, f32[]{:T(128)} %constant.37.clone.1), dimensions={0}, to_apply=%region_3.6 | reduce | flops 14221312 | bytes 59637764 | tf_op jit(solution)/shard_map/reduce_sum | solution.py:12
  438.1 0.6 fusion.4
  438.8 38.4 %psum.15 = f32[32,32]{0,1:T(8,128)S(1)} all-reduce(f32[32,32]{0,1:T(8,128)S(1)} %fusion.25), channel_id=1, replica_groups=mesh['rep'=1,'fsdp'=32] {'fsdp'}, use_global_device_ids=true, to_apply=%region_4.7 | all-reduce | flops 1024 | bytes 8192 | tf_op jit(solution)/shard_map/psum | solution.py:21
  477.4 2.9 cholesky.55
  480.3 0.6 compare_reduce_fusion
  481.0 0.7 fusion.14
  481.6 2.4 custom-call.7
  484.3 1.6 fusion.2
  486.0 316.0 %all-gather.8.cloned.1.call-done = f32[1024,14336]{1,0:T(8,128)} async-done(((f32[32,14336]{1,0:T(8,128)}), f32[1024,14336]{1,0:T(8,128)}) %all-gather.8.cloned.1.call-update) | async-done | bytes 58720272 | tf_op jit(solution)/shard_map/all_gather | solution.py:12
  801.9 19.6 %reduce_sum.19 = f32[32,14336]{1,0:T(8,128)} reduce(f32[32,32,14336]{2,1,0:T(8,128)} %bitcast.54, f32[]{:T(128)} %constant.37.clone.1), dimensions={0}, to_apply=%region_5.8 | reduce | flops 14221312 | bytes 60555268 | tf_op jit(solution)/shard_map/reduce_sum | solution.py:12
  821.6 3.4 fusion.1
  825.0 1.6 constant_dynamic-slice_fusion
  (17 shorter events, 0.9 us)
Async XLA Ops:
  7.2 412.4 %all-gather.6.cloned.1.call-start = ((), (), s32[]{:S(2)}) async-start(), calls=%async_computation | async-start | bytes 60555264 | tf_op jit(solution)/shard_map/all_gather | solution.py:12
  53.7 2.7 copy-start
  103.9 698.0 %all-gather.8.cloned.1.call-start = ((), (), s32[]{:S(2)}) async-start(), calls=%async_computation.1 | async-start | bytes 60555264 | tf_op jit(solution)/shard_map/all_gather | solution.py:12
  484.3 337.3 %copy-start.1 = (f32[64,32]{0,1:T(8,128)}, f32[64,32]{0,1:T(8,128)S(1)}, u32[]{:S(2)}) copy-start(f32[64,32]{0,1:T(8,128)S(1)} %convolution_bitcast_fusion) | copy-start | bytes 24580
Sparse Core Ops, SparseCore 0:
  104.0 315.5 all-gather.5
  486.1 315.8 all-gather.7
